TPU v7x, 128 devices: a whole 4x4x4 slice. The times are simulated.
128 devices in a mesh: row: 8 (over y, z_lo), col: 16 (over z_hi, x, core).
Axes of the slice: x: 4, y: 4, z: 4 (z_hi: 2, z_lo: 2; z = z_hi * 2 + z_lo), core: 2. Of those that a mesh axis runs over, the one named last changes fastest.
Arguments:
- spectra: bfloat16 [16, 2048, 2048], P('row', None, 'col'), may hold values from -6 to 6
- coupling: float32 [16], replicated, may hold values from 0.2 to 1
Outputs:
- returned_spectra: bfloat16 [16, 2048, 2048], P('row', None, 'col')
All inputs are finite; a program needn't handle non-finite values.
Results may differ from a plain program's by a relative error of at most 0.0079.
Values may be sent and summed in bfloat16 or wider, within the bound.
A program may use at most 128 MiB of HBM per device.

v0:
```python
import math
import jax
import jax.numpy as jnp
from jax import lax
from jax.sharding import Mesh
from jax.sharding import PartitionSpec as P

NX = 3072
NY = 3072
M = 1024
COL = ("col_0", "col_1", "col_2")


def in_blocks(array, dim, peers):
    dims = array.shape
    tiles = array.reshape(*dims[:dim], peers, dims[dim] // peers, *dims[dim + 1 :])
    return jnp.moveaxis(tiles, dim, 0)


def joined_along(tiles, dim):
    dims = list(tiles.shape[1:])
    dims[dim] *= tiles.shape[0]
    return jnp.moveaxis(tiles, 0, dim).reshape(dims)


def moved_by_axis(tiles, axes, turns):
    dims = [lax.axis_size(a) for a in axes]
    tiles = tiles.reshape(*dims, *tiles.shape[1:])
    for k in turns:
        tiles = lax.all_to_all(tiles, axes[k], split_axis=k, concat_axis=k, tiled=True)
    return tiles.reshape(-1, *tiles.shape[len(axes) :])


def core_and_chips(array, groups, turns, split_dim, concat_dim):
    peers = lax.axis_size(groups[0]) * lax.axis_size(groups[1])
    tiles = in_blocks(array, split_dim, peers)
    return joined_along(moved_by_axis(tiles, groups, turns), concat_dim)


def fourier_rows(mode_count, length, factor):
    wavenumber = jnp.arange(1, mode_count + 1, dtype=jnp.int32)
    position = jnp.arange(length, dtype=jnp.int32)
    residue = wavenumber[:, None] * position[None, :] % length
    angles = residue.astype(jnp.float32) * (2.0 * math.pi / length)
    table = jnp.concatenate([jnp.cos(angles), jnp.sin(angles)], 0) * factor
    return table.astype(jnp.bfloat16)


def ellipse(row_index, column_index, mode_count):
    row_waves = row_index % mode_count + 1
    col_waves = column_index % mode_count + 1
    inside = (
        row_waves[:, None] * row_waves[:, None] + col_waves[None, :] * col_waves[None, :]
        <= mode_count * mode_count
    )
    return inside.astype(jnp.float32)


def on_device(spectra, coupling):
    local_count = spectra.shape[0]
    width_here = spectra.shape[2]
    inverse_y = fourier_rows(M, NY, 1.0 / math.sqrt(M)).T
    inverse_x = fourier_rows(M, NX, 1.0 / math.sqrt(M))
    forward_x = fourier_rows(M, NX, 2.0 * math.sqrt(M) / NX).T
    forward_y = fourier_rows(M, NY, 2.0 * math.sqrt(M) / NY)
    half_done = jnp.einsum(
        "yk,fkc->fyc", inverse_y, spectra, preferred_element_type=jnp.float32
    ).astype(jnp.bfloat16)
    gathered = core_and_chips(half_done, (("col_0", "col_1"), "col_2"), (1, 0), 1, 2)
    first_field = lax.axis_index("row") * local_count
    strength = lax.dynamic_slice_in_dim(coupling, first_field, gathered.shape[0])
    gridded = jnp.einsum("fyk,kx->fyx", gathered, inverse_x, preferred_element_type=jnp.float32)
    tendency = (gridded + strength[:, None, None] * gridded * gridded).astype(jnp.bfloat16)
    projected = jnp.einsum(
        "fyx,xk->fyk", tendency, forward_x, preferred_element_type=jnp.float32
    ).astype(jnp.bfloat16)
    returned = lax.all_to_all(projected, COL, split_axis=2, concat_axis=1, tiled=True)
    result = jnp.einsum("ky,fyc->fkc", forward_y, returned, preferred_element_type=jnp.float32)
    columns = lax.axis_index(COL) * width_here + jnp.arange(width_here, dtype=jnp.int32)
    inside = ellipse(jnp.arange(2 * M, dtype=jnp.int32), columns, M)
    return (result * inside[None, :, :]).astype(jnp.bfloat16)


def solution(mesh):
    torus = Mesh(
        mesh.devices.reshape(mesh.shape["row"], 2, 4, 2), ("row", "col_0", "col_1", "col_2")
    )
    return jax.shard_map(
        on_device,
        mesh=torus,
        in_specs=(P("row", None, COL), P()),
        out_specs=P("row", None, COL),
        check_vma=False,
    )
```

profile of v0, /device:TPU:1, one launch (start us, length us, event | category | flops | bytes accessed | tf_op | source)
XLA Modules:
  0.0 182.3 jit_solution(15126641113345682228)
XLA Ops:
  0.0 0.0 copy-start
  0.0 52.6 %fusion.7 = (f32[1024,3072]{0,1:T(8,128)}, f32[1024,3072]{0,1:T(8,128)}) fusion(s32[1024]{0:T(1024)S(1)} %iota_add_fusion), kind=kLoop, calls=%fused_computation.12 | loop fusion | flops 28311552 | bytes 25169920 | tf_op jit(solution)/shard_map/cos | solution.py:45
  52.6 0.0 copy-done
  52.6 10.0 %convolution_convert_fusion = bf16[3072,2,128]{2,0,1:T(8,128)(2,1)S(1)} fusion(bf16[2,2048,128]{2,1,0:T(8,128)(2,1)S(1)} %copy-done, f32[1024,3072]{0,1:T(8,128)} %get-tuple-element.6, f32[1024,3072]{0,1:T(8,128)} %get-tuple-element.5), kind=kOutput, calls=%fused_computation.16 | convolution fusion | flops 3240886272 | bytes 27787264 | tf_op jit(solution)/shard_map/yk,fkc->fyc/dot_general | solution.py:66
  62.6 0.0 copy-start.1
  62.6 0.1 copy.24
  62.8 6.0 %all_to_all.28 = bf16[8,2,2,192,128]{4,3,0,2,1:T(8,128)(2,1)S(1)} all-to-all(bf16[8,2,2,192,128]{4,3,0,2,1:T(8,128)(2,1)S(1)} %copy.24), channel_id=1, replica_groups=mesh['row'=8,'col_0'=2,'col_1'=4,'col_2'=2] {'col_2'}, dimensions={1} | all-to-all | bytes 3145728 | tf_op jit(solution)/shard_map/all_to_all | solution.py:30
  68.8 1.3 copy.25
  70.1 7.4 %all-to-all-start.1 = ((bf16[8,2,2,192,128]{4,3,1,2,0:T(8,128)(2,1)}), bf16[8,2,2,192,128]{4,3,1,2,0:T(8,128)(2,1)S(1)}, u32[]{:S(2)}, u32[]{:S(2)}) async-start(bf16[8,2,2,192,128]{4,3,1,2,0:T(8,128)(2,1)} %copy.25), calls=%async_computation.1 | async-start | bytes 3145728 | tf_op jit(solution)/shard_map/all_to_all | solution.py:30
  77.6 0.0 copy-done.1
  77.6 0.1 dynamic_slice.3
  77.7 22.9 %all-to-all-done.1 = bf16[8,2,2,192,128]{4,3,1,2,0:T(8,128)(2,1)S(1)} async-done(((bf16[8,2,2,192,128]{4,3,1,2,0:T(8,128)(2,1)}), bf16[8,2,2,192,128]{4,3,1,2,0:T(8,128)(2,1)S(1)}, u32[]{:S(2)}, u32[]{:S(2)}) %all-to-all-start.1) | async-done | bytes 1572896 | tf_op jit(solution)/shard_map/all_to_all | solution.py:30
  100.6 1.3 copy.26
  101.8 12.3 %fusion.9 = bf16[2,192,3072]{2,1,0:T(8,128)(2,1)} fusion(f32[2]{0:T(128)S(1)} %dynamic_slice.3, f32[1024,3072]{0,1:T(8,128)} %get-tuple-element.6, f32[1024,3072]{0,1:T(8,128)} %get-tuple-element.5, bf16[16,2,24,8,128]{4,3,2,1,0:T(8,128)(2,1)} %bitcast.40), kind=kOutput, calls=%fused_computation.15 | convolution fusion | flops 4855431168 | bytes 29097992 | tf_op jit(solution)/shard_map/fyk,kx->fyx/dot_general | solution.py:72
  114.1 13.9 %convolution_convert_fusion.1 = bf16[2,192,2048]{2,1,0:T(8,128)(2,1)S(1)} fusion(bf16[2,192,3072]{2,1,0:T(8,128)(2,1)} %fusion.9, f32[1024,3072]{0,1:T(8,128)} %get-tuple-element.6, f32[1024,3072]{0,1:T(8,128)} %get-tuple-element.5), kind=kOutput, calls=%fused_computation.17 | convolution fusion | flops 4851499008 | bytes 29097984 | tf_op jit(solution)/shard_map/fyx,xk->fyk/dot_general | solution.py:74
  128.1 3.8 %copy.30 = bf16[2,192,2048]{1,0,2:T(2,128)(2,1)} copy(bf16[2,192,2048]{2,1,0:T(8,128)(2,1)S(1)} %convolution_convert_fusion.1) | data formatting | bytes 3145728 | tf_op jit(solution)/shard_map/convert_element_type | solution.py:76
  131.9 4.6 %all-to-all-start.2 = ((bf16[2,192,2048]{1,0,2:T(2,128)(2,1)}), bf16[2,192,2048]{1,0,2:T(2,128)(2,1)S(1)}, u32[]{:S(2)}, u32[]{:S(2)}) async-start(bf16[2,192,2048]{1,0,2:T(2,128)(2,1)} %copy.30), calls=%async_computation.2 | async-start | bytes 4194304 | tf_op jit(solution)/shard_map/all_to_all | solution.py:77
  136.5 1.1 fusion.18
  137.7 27.3 %all-to-all-done.2 = bf16[2,192,2048]{1,0,2:T(2,128)(2,1)S(1)} async-done(((bf16[2,192,2048]{1,0,2:T(2,128)(2,1)}), bf16[2,192,2048]{1,0,2:T(2,128)(2,1)S(1)}, u32[]{:S(2)}, u32[]{:S(2)}) %all-to-all-start.2) | async-done | bytes 1572896 | tf_op jit(solution)/shard_map/all_to_all | solution.py:77
  165.0 3.7 %copy.44 = bf16[2,192,16,128]{3,1,2,0:T(8,128)(2,1)} copy(bf16[2,192,16,128]{1,0,3,2:T(2,128)(2,1)S(1)} %bitcast.38) | data formatting | bytes 3145728 | tf_op jit(solution)/shard_map/all_to_all | solution.py:77
  168.7 12.3 %fusion.11 = bf16[2,2048,128]{1,2,0:T(8,128)(2,1)S(1)} fusion(bf16[2,3072,128]{2,1,0:T(8,128)(2,1)} %bitcast.39, f32[1024,3072]{0,1:T(8,128)} %get-tuple-element.6, f32[1024,3072]{0,1:T(8,128)} %get-tuple-element.5, f32[2048,128]{0,1:T(8,128)} %fusion.18), kind=kOutput, calls=%fused_computation.20 | convolution fusion | flops 3241148416 | bytes 28835840 | tf_op jit(solution)/shard_map/ky,fyc->fkc/dot_general | solution.py:78
  181.0 1.3 copy.35
  (3 shorter events, 0.0 us)
Async XLA Ops:
  0.0 52.6 %copy-start = (bf16[2,2048,128]{2,1,0:T(8,128)(2,1)S(1)}, bf16[2,2048,128]{2,1,0:T(8,128)(2,1)}, u32[]{:S(2)}) copy-start(bf16[2,2048,128]{2,1,0:T(8,128)(2,1)} %param.2) | copy-start | bytes 3145732
  62.6 14.9 %copy-start.1 = (f32[16]{0:T(128)S(1)}, f32[16]{0:T(128)}, u32[]{:S(2)}) copy-start(f32[16]{0:T(128)} %param.3) | copy-start | bytes 196
  70.1 30.4 %all-to-all-start.1 = ((bf16[8,2,2,192,128]{4,3,1,2,0:T(8,128)(2,1)}), bf16[8,2,2,192,128]{4,3,1,2,0:T(8,128)(2,1)S(1)}, u32[]{:S(2)}, u32[]{:S(2)}) async-start(bf16[8,2,2,192,128]{4,3,1,2,0:T(8,128)(2,1)} %copy.25), calls=%async_computation.1 | async-start | bytes 3145728 | tf_op jit(solution)/shard_map/all_to_all | solution.py:30
  131.9 33.1 %all-to-all-start.2 = ((bf16[2,192,2048]{1,0,2:T(2,128)(2,1)}), bf16[2,192,2048]{1,0,2:T(2,128)(2,1)S(1)}, u32[]{:S(2)}, u32[]{:S(2)}) async-start(bf16[2,192,2048]{1,0,2:T(2,128)(2,1)} %copy.30), calls=%async_computation.2 | async-start | bytes 4194304 | tf_op jit(solution)/shard_map/all_to_all | solution.py:77
where the time goes:
time: 183 us; the launch traced here: 182 us
  other arithmetic  53.8 us (29%)
  waiting for transfers between devices  50.2 us (27%)
  matrix products  48.6 us (27%)
  starting transfers between devices  12.1 us (7%)
  local copies, waits for them, and re-layouts  11.6 us (6%)
  blocking collectives  6 us (3%)
    cos x1, other arithmetic, fourier_rows(): table = jnp.concatenate([jnp.cos(angles), jnp.sin(angles)], 0) * factor  52.6 us
    all_to_all x1, waiting for transfers between devices, on_device(): lax.all_to_all(projected, COL, split_axis=2, concat_axis=1, tiled=True)  27.3 us
    all_to_all x1, waiting for transfers between devices, moved_by_axis(): lax.all_to_all(tiles, axes[k], split_axis=k, concat_axis=k, tiled=True)  22.9 us
    dot_general x1, matrix products, on_device(): jnp.einsum('fyx,xk->fyk', tendency, forward_x, preferred_element_type=jnp...  13.9 us
    dot_general x1, matrix products, on_device(): jnp.einsum('fyk,kx->fyx', gathered, inverse_x, preferred_element_type=jnp...  12.3 us
    dot_general x1, matrix products, on_device(): jnp.einsum('ky,fyc->fkc', forward_y, returned, preferred_element_type=jnp...  12.3 us
    dot_general x1, matrix products, on_device(): jnp.einsum('yk,fkc->fyc', inverse_y, spectra, preferred_element_type=jnp....  10 us
    all_to_all x1, starting transfers between devices, moved_by_axis(): lax.all_to_all(tiles, axes[k], split_axis=k, concat_axis=k, tiled=True)  7.45 us
  transfers between devices with their start and end apart: 2, of which 2 were waited for; matrix products, arithmetic and copies ran while one was open for 1% of the time, Pallas kernels for 0%

commit v1 on v0

--- a/solution.py
+++ b/solution.py
@@ -74,7 +74,10 @@
     projected = jnp.einsum(
         "fyx,xk->fyk", tendency, forward_x, preferred_element_type=jnp.float32
     ).astype(jnp.bfloat16)
-    returned = lax.all_to_all(projected, COL, split_axis=2, concat_axis=1, tiled=True)
+    returned = jnp.concatenate(
+        lax.all_to_all(jnp.stack(jnp.split(projected, lax.axis_size(COL), axis=2)), COL, 0, 0),
+        axis=1,
+    )
     result = jnp.einsum("ky,fyc->fkc", forward_y, returned, preferred_element_type=jnp.float32)
     columns = lax.axis_index(COL) * width_here + jnp.arange(width_here, dtype=jnp.int32)
     inside = ellipse(jnp.arange(2 * M, dtype=jnp.int32), columns, M)

time: 183 us -> 182 us (level)
  waiting for transfers between devices: 50.2 us -> 44.6 us
  local copies, waits for them, and re-layouts: 11.6 us -> 16.1 us
    unnamed x4 -> x19, local copies, waits for them, and re-layouts: 0.01 us -> 9.99 us
    all_to_all x1, waiting for transfers between devices: 27.3 us -> 21.7 us  [on_device(): lax.all_to_all(jnp.stack(jnp.split(projected, lax.axis_size(COL), axis=2)...]
    convert_element_type x1 -> x0, local copies, waits for them, and re-layouts: 3.83 us -> none  [on_device(): projected = jnp.einsum('fyx,xk->fyk', tendency, forward_x, preferred_elem...]
    all_to_all x1 -> x0, local copies, waits for them, and re-layouts: 3.66 us -> none  [on_device(): lax.all_to_all(projected, COL, split_axis=2, concat_axis=1, tiled=True)]
where the time goes in v1:
time: 182 us; the launch traced here: 181 us
  other arithmetic  53.8 us (30%)
  matrix products  48.6 us (27%)
  waiting for transfers between devices  44.6 us (25%)
  local copies, waits for them, and re-layouts  16.1 us (9%)
  starting transfers between devices  12.2 us (7%)
  blocking collectives  6 us (3%)
    cos x1, other arithmetic, fourier_rows(): table = jnp.concatenate([jnp.cos(angles), jnp.sin(angles)], 0) * factor  52.6 us
    all_to_all x1, waiting for transfers between devices, moved_by_axis(): lax.all_to_all(tiles, axes[k], split_axis=k, concat_axis=k, tiled=True)  22.9 us
    all_to_all x1, waiting for transfers between devices, on_device(): lax.all_to_all(jnp.stack(jnp.split(projected, lax.axis_size(COL), axis=2)...  21.7 us
    dot_general x1, matrix products, on_device(): jnp.einsum('fyx,xk->fyk', tendency, forward_x, preferred_element_type=jnp...  13.9 us
    dot_general x1, matrix products, on_device(): jnp.einsum('fyk,kx->fyx', gathered, inverse_x, preferred_element_type=jnp...  12.3 us
    dot_general x1, matrix products, on_device(): jnp.einsum('ky,fyc->fkc', forward_y, returned, preferred_element_type=jnp...  12.3 us
    dot_general x1, matrix products, on_device(): jnp.einsum('yk,fkc->fyc', inverse_y, spectra, preferred_element_type=jnp....  10 us
    unnamed x19, local copies, waits for them, and re-layouts  9.99 us
  transfers between devices with their start and end apart: 2, of which 2 were waited for; matrix products, arithmetic and copies ran while one was open for 1% of the time, Pallas kernels for 0%

profile of v1, /device:TPU:1, one launch (start us, length us, event | category | flops | bytes accessed | tf_op | source)
XLA Modules:
  0.0 181.3 jit_solution(3998821557926078322)
XLA Ops:
  0.0 52.6 %fusion.7 = (f32[1024,3072]{0,1:T(8,128)}, f32[1024,3072]{0,1:T(8,128)}) fusion(s32[1024]{0:T(1024)S(1)} %iota_add_fusion), kind=kLoop, calls=%fused_computation.12 | loop fusion | flops 28311552 | bytes 25169920 | tf_op jit(solution)/shard_map/cos | solution.py:45
  52.6 10.0 %convolution_convert_fusion = bf16[3072,2,128]{2,0,1:T(8,128)(2,1)S(1)} fusion(bf16[2,2048,128]{2,1,0:T(8,128)(2,1)S(1)} %copy-done, f32[1024,3072]{0,1:T(8,128)} %get-tuple-element.6, f32[1024,3072]{0,1:T(8,128)} %get-tuple-element.5), kind=kOutput, calls=%fused_computation.16 | convolution fusion | flops 3240886272 | bytes 27787264 | tf_op jit(solution)/shard_map/yk,fkc->fyc/dot_general | solution.py:66
  62.8 6.0 %all_to_all.15 = bf16[8,2,2,192,128]{4,3,0,2,1:T(8,128)(2,1)S(1)} all-to-all(bf16[8,2,2,192,128]{4,3,0,2,1:T(8,128)(2,1)S(1)} %copy.23), channel_id=1, replica_groups=mesh['row'=8,'col_0'=2,'col_1'=4,'col_2'=2] {'col_2'}, dimensions={1} | all-to-all | bytes 3145728 | tf_op jit(solution)/shard_map/all_to_all | solution.py:30
  68.8 1.3 copy.24
  70.1 7.6 %all-to-all-start.1 = ((bf16[8,2,2,192,128]{4,3,1,2,0:T(8,128)(2,1)}), bf16[8,2,2,192,128]{4,3,1,2,0:T(8,128)(2,1)S(1)}, u32[]{:S(2)}, u32[]{:S(2)}) async-start(bf16[8,2,2,192,128]{4,3,1,2,0:T(8,128)(2,1)} %copy.24), calls=%async_computation.1 | async-start | bytes 3145728 | tf_op jit(solution)/shard_map/all_to_all | solution.py:30
  77.8 22.9 %all-to-all-done.1 = bf16[8,2,2,192,128]{4,3,1,2,0:T(8,128)(2,1)S(1)} async-done(((bf16[8,2,2,192,128]{4,3,1,2,0:T(8,128)(2,1)}), bf16[8,2,2,192,128]{4,3,1,2,0:T(8,128)(2,1)S(1)}, u32[]{:S(2)}, u32[]{:S(2)}) %all-to-all-start.1) | async-done | bytes 1572896 | tf_op jit(solution)/shard_map/all_to_all | solution.py:30
  100.7 1.3 copy.25
  101.9 12.3 %fusion.9 = bf16[2,192,3072]{2,1,0:T(8,128)(2,1)} fusion(f32[2]{0:T(128)S(1)} %dynamic_slice.3, f32[1024,3072]{0,1:T(8,128)} %get-tuple-element.6, f32[1024,3072]{0,1:T(8,128)} %get-tuple-element.5, bf16[16,2,24,8,128]{4,3,2,1,0:T(8,128)(2,1)} %bitcast.101), kind=kOutput, calls=%fused_computation.15 | convolution fusion | flops 4855431168 | bytes 29097992 | tf_op jit(solution)/shard_map/fyk,kx->fyx/dot_general | solution.py:72
  114.3 13.9 %convolution_convert_fusion.1 = bf16[2,192,2048]{2,1,0:T(8,128)(2,1)S(1)} fusion(bf16[2,192,3072]{2,1,0:T(8,128)(2,1)} %fusion.9, f32[1024,3072]{0,1:T(8,128)} %get-tuple-element.6, f32[1024,3072]{0,1:T(8,128)} %get-tuple-element.5), kind=kOutput, calls=%fused_computation.17 | convolution fusion | flops 4851499008 | bytes 29097984 | tf_op jit(solution)/shard_map/fyx,xk->fyk/dot_general | solution.py:74
  130.8 0.7 fusion.30
  132.2 0.7 fusion.28
  132.8 0.7 fusion.27
  133.5 0.7 fusion.26
  134.8 0.7 fusion.24
  135.5 0.7 fusion.23
  136.2 0.7 fusion.22
  136.8 0.7 fusion.21
  137.5 0.7 fusion.20
  138.8 4.6 %all-to-all-start.2 = ((bf16[16,2,192,128]{3,2,1,0:T(8,128)(2,1)}), bf16[16,2,192,128]{3,2,1,0:T(8,128)(2,1)S(1)}, u32[]{:S(2)}, u32[]{:S(2)}) async-start(bf16[16,2,192,128]{3,2,1,0:T(8,128)(2,1)} %fusion.19), calls=%async_computation.2 | async-start | bytes 3145728 | tf_op jit(solution)/shard_map/all_to_all | solution.py:78
  143.5 1.1 fusion.18
  144.6 21.7 %all-to-all-done.2 = bf16[16,2,192,128]{3,2,1,0:T(8,128)(2,1)S(1)} async-done(((bf16[16,2,192,128]{3,2,1,0:T(8,128)(2,1)}), bf16[16,2,192,128]{3,2,1,0:T(8,128)(2,1)S(1)}, u32[]{:S(2)}, u32[]{:S(2)}) %all-to-all-start.2) | async-done | bytes 1572896 | tf_op jit(solution)/shard_map/all_to_all | solution.py:78
  166.3 1.3 copy.29
  167.7 12.3 %fusion.11 = bf16[2,2048,128]{1,2,0:T(8,128)(2,1)S(1)} fusion(bf16[2,3072,128]{2,1,0:T(8,128)(2,1)} %bitcast.100, f32[1024,3072]{0,1:T(8,128)} %get-tuple-element.6, f32[1024,3072]{0,1:T(8,128)} %get-tuple-element.5, f32[2048,128]{0,1:T(8,128)} %fusion.18), kind=kOutput, calls=%fused_computation.20 | convolution fusion | flops 3241148416 | bytes 28835840 | tf_op jit(solution)/shard_map/ky,fyc->fkc/dot_general | solution.py:81
  180.0 1.3 copy.32
  (16 shorter events, 4.8 us)
Async XLA Ops:
  0.0 52.6 %copy-start = (bf16[2,2048,128]{2,1,0:T(8,128)(2,1)S(1)}, bf16[2,2048,128]{2,1,0:T(8,128)(2,1)}, u32[]{:S(2)}) copy-start(bf16[2,2048,128]{2,1,0:T(8,128)(2,1)} %param.2) | copy-start | bytes 3145732
  70.1 7.6 %copy-start.1 = (f32[16]{0:T(128)S(1)}, f32[16]{0:T(128)}, u32[]{:S(2)}) copy-start(f32[16]{0:T(128)} %param.3) | copy-start | bytes 196
  70.1 30.6 %all-to-all-start.1 = ((bf16[8,2,2,192,128]{4,3,1,2,0:T(8,128)(2,1)}), bf16[8,2,2,192,128]{4,3,1,2,0:T(8,128)(2,1)S(1)}, u32[]{:S(2)}, u32[]{:S(2)}) async-start(bf16[8,2,2,192,128]{4,3,1,2,0:T(8,128)(2,1)} %copy.24), calls=%async_computation.1 | async-start | bytes 3145728 | tf_op jit(solution)/shard_map/all_to_all | solution.py:30
  138.8 27.5 %all-to-all-start.2 = ((bf16[16,2,192,128]{3,2,1,0:T(8,128)(2,1)}), bf16[16,2,192,128]{3,2,1,0:T(8,128)(2,1)S(1)}, u32[]{:S(2)}, u32[]{:S(2)}) async-start(bf16[16,2,192,128]{3,2,1,0:T(8,128)(2,1)} %fusion.19), calls=%async_computation.2 | async-start | bytes 3145728 | tf_op jit(solution)/shard_map/all_to_all | solution.py:78
